TPU v7x, 32 devices: a whole 2x2x4 slice. The times are simulated.
32 devices in a mesh: blk: 4 (over x, core), vox: 8 (over z, y).
Axes of the slice: x: 2, y: 2, z: 4, core: 2. Of those that a mesh axis runs over, the one named last changes fastest.
Arguments:
- src_fields: bfloat16 [256, 32768], P('blk', 'vox'), may hold values from -6 to 6
- det_fields: bfloat16 [256, 32768], P('blk', 'vox'), may hold values from -6 to 6
- probes: bfloat16 [2, 32768], P(None, 'vox'), may hold values from -6 to 6
Outputs:
- curvature: float32 [2, 32768], P(None, 'vox')
All inputs are finite; a program needn't handle non-finite values.
Results may differ from a plain program's by a relative error of at most 0.0016.
Values may be sent and summed in bfloat16 or wider, within the bound.
No kernel may reach another device: no remote copies, remote signals or barrier semaphores. Data moves between devices by JAX's collectives and lax.ppermute only.
A program may use at most 64 MiB of HBM per device.

v0:
```python
import jax
import jax.numpy as jnp
from jax import lax
from jax.sharding import PartitionSpec as P


def shards(src_fields, det_fields, probes):
    src_count, vox_count = src_fields.shape
    det_count = det_fields.shape[0]
    groups = lax.axis_size("blk")
    det_total = det_count * groups
    probe_count = probes.shape[0]
    weighted = (src_fields.astype(jnp.float32)[None] * probes.astype(jnp.float32)[:, None]).astype(
        jnp.bfloat16
    )
    weighted = weighted.reshape(probe_count * src_count, vox_count)
    slab = jnp.zeros((0, vox_count), jnp.bfloat16)
    product = jnp.einsum(
        "rv,dv->rd",
        weighted,
        lax.all_gather(det_fields, "blk", axis=0, tiled=True),
        preferred_element_type=jnp.float32,
    )
    partial_value, slab = (product, slab)
    measured = lax.psum(partial_value, "vox")
    measured_b = measured.astype(jnp.bfloat16)
    backproj = jnp.dot(
        measured_b,
        lax.all_gather(det_fields, "blk", axis=0, tiled=True),
        preferred_element_type=jnp.float32,
    )
    backproj = backproj.reshape(probe_count, src_count, vox_count)
    contrib = jnp.sum(src_fields.astype(jnp.float32)[None] * backproj, axis=1)
    total = lax.psum(contrib, "blk")
    normalizer = jnp.float32(1.0 / (src_count * groups * det_total))
    return total * normalizer


def solution(mesh):
    return jax.shard_map(
        shards,
        mesh=mesh,
        in_specs=(P("blk", "vox"), P("blk", "vox"), P(None, "vox")),
        out_specs=P(None, "vox"),
        check_vma=False,
    )
```

profile of v0, /device:TPU:0, one launch (start us, length us, event | category | flops | bytes accessed | tf_op | source)
XLA Modules:
  0.0 93.9 jit_solution(10206651195195280861)
XLA Ops:
  6.5 0.0 all-gather.2.cloned.1.call-start
  6.5 0.7 all-gather.2.cloned.1.call-update
  7.3 0.7 convert_element_type.18
  8.0 1.1 %convert_element_type.17 = f32[64,4096]{1,0:T(8,128)S(1)} convert(bf16[64,4096]{1,0:T(8,128)(2,1)} %param.3) | non-fusion elementwise | flops 262144 | bytes 1572864 | tf_op jit(solution)/shard_map/convert_element_type | solution.py:33
  9.1 1.1 %multiply_convert_fusion = bf16[2,64,4096]{2,1,0:T(8,128)(2,1)} fusion(f32[2,4096]{1,0:T(2,128)S(1)} %convert_element_type.18, f32[64,4096]{1,0:T(8,128)S(1)} %convert_element_type.17), kind=kLoop, calls=%fused_computation.1 | loop fusion | flops 1048576 | bytes 2129920 | tf_op jit(solution)/shard_map/convert_element_type | solution.py:13
  10.3 24.0 %all-gather.2.cloned.1.call-done = bf16[256,4096]{1,0:T(8,128)(2,1)} async-done(((bf16[64,4096]{1,0:T(8,128)(2,1)}), bf16[256,4096]{1,0:T(8,128)(2,1)}) %all-gather.2.cloned.1.call-update) | async-done | bytes 2097168 | tf_op jit(solution)/shard_map/all_gather | solution.py:21
  34.2 0.0 copy-start
  34.2 2.9 %fusion.2 = f32[128,256]{1,0:T(8,128)S(1)} fusion(bf16[128,4096]{1,0:T(8,128)(2,1)} %bitcast.7, bf16[256,4096]{1,0:T(8,128)(2,1)} %all-gather.2.cloned.1.call-done), kind=kOutput, calls=%fused_computation.5 | convolution fusion | flops 268435456 | bytes 3276800 | tf_op jit(solution)/shard_map/rv,dv->rd/dot_general | solution.py:18
  37.1 38.3 %all-reduce.1 = bf16[128,256]{1,0:T(8,128)(2,1)S(1)} all-reduce(f32[128,256]{1,0:T(8,128)S(1)} %fusion.2), channel_id=1, replica_groups=mesh['blk'=4,'vox'=8] {'vox'}, use_global_device_ids=true, to_apply=%region_0.0 | all-reduce | flops 32768 | bytes 196608 | tf_op jit(solution)/shard_map/psum | solution.py:25
  75.5 0.0 copy-done
  75.5 0.5 multiply_reduce_fusion
  76.0 10.4 %psum.15 = f32[2,4096]{1,0:T(2,128)S(1)} all-reduce(f32[2,4096]{1,0:T(2,128)S(1)} %multiply_reduce_fusion), channel_id=1, replica_groups=mesh['blk'=4,'vox'=8] {'blk'}, use_global_device_ids=true, to_apply=%region_2.0 | all-reduce | flops 8192 | bytes 65536 | tf_op jit(solution)/shard_map/psum | solution.py:34
  86.4 0.6 broadcast_multiply_fusion
Async XLA Ops:
  6.5 27.7 %all-gather.2.cloned.1.call-start = ((), (), s32[]{:S(2)}) async-start(), calls=%async_computation | async-start | bytes 2621440 | tf_op jit(solution)/shard_map/all_gather | solution.py:21
  34.2 41.2 %copy-start = (bf16[256,4096]{1,0:T(8,128)(2,1)S(1)}, bf16[256,4096]{1,0:T(8,128)(2,1)}, u32[]{:S(2)}) copy-start(bf16[256,4096]{1,0:T(8,128)(2,1)} %all-gather.2.cloned.1.call-done) | copy-start | bytes 6291460
Sparse Core Ops, SparseCore 0:
  8.9 25.2 all-gather.1
where the time goes:
time: 94.1 us; the launch traced here: 93.9 us
  blocking collectives  48.8 us (52%)
  waiting for transfers between devices  24.7 us (26%)
  between operations  13.4 us (14%)
  other arithmetic  3.62 us (4%)
  matrix products  3.39 us (4%)
    psum x1, blocking collectives, shards(): measured = lax.psum(partial_value, 'vox')  38.3 us
    all_gather x1, waiting for transfers between devices, shards(): lax.all_gather(det_fields, 'blk', axis=0, tiled=True)  24 us
    psum x1, blocking collectives, shards(): total = lax.psum(contrib, 'blk')  10.4 us
    dot_general x1, matrix products, shards(): jnp.einsum('rv,dv->rd', weighted, lax.all_gather(det_fields, 'blk', axis=...  2.89 us
  transfers between devices with their start and end apart: 1, of which 1 were waited for; matrix products, arithmetic and copies ran while one was open for 3% of the time, Pallas kernels for 0%

commit v1 on v0

--- a/solution.py
+++ b/solution.py
@@ -31,7 +31,7 @@
     )
     backproj = backproj.reshape(probe_count, src_count, vox_count)
     contrib = jnp.sum(src_fields.astype(jnp.float32)[None] * backproj, axis=1)
-    total = lax.psum(contrib, "blk")
+    total = jnp.sum(lax.all_gather(contrib, "blk"), axis=0)
     normalizer = jnp.float32(1.0 / (src_count * groups * det_total))
     return total * normalizer
 

time: 94.1 us -> 89.2 us (0.948)
  blocking collectives: 48.8 us -> 43.8 us
    psum x1 -> x0, blocking collectives: 10.4 us -> none  [shards(): total = lax.psum(contrib, 'blk')]
    all_gather x0 -> x1, blocking collectives: none -> 5.42 us  [shards(): total = jnp.sum(lax.all_gather(contrib, 'blk'), axis=0)]
where the time goes in v1:
time: 89.2 us; the launch traced here: 88.9 us
  blocking collectives  43.8 us (49%)
  waiting for transfers between devices  24.7 us (28%)
  between operations  13.4 us (15%)
  other arithmetic  3.67 us (4%)
  matrix products  3.39 us (4%)
    psum x1, blocking collectives, shards(): measured = lax.psum(partial_value, 'vox')  38.3 us
    all_gather x1, waiting for transfers between devices, shards(): lax.all_gather(det_fields, 'blk', axis=0, tiled=True)  24 us
    all_gather x1, blocking collectives, shards(): total = jnp.sum(lax.all_gather(contrib, 'blk'), axis=0)  5.42 us
    dot_general x1, matrix products, shards(): jnp.einsum('rv,dv->rd', weighted, lax.all_gather(det_fields, 'blk', axis=...  2.89 us
  transfers between devices with their start and end apart: 1, of which 1 were waited for; matrix products, arithmetic and copies ran while one was open for 3% of the time, Pallas kernels for 0%

profile of v1, /device:TPU:0, one launch (start us, length us, event | category | flops | bytes accessed | tf_op | source)
XLA Modules:
  0.0 88.9 jit_solution(7705705265304068397)
XLA Ops:
  6.5 0.0 all-gather.4.cloned.1.call-start
  6.5 0.7 all-gather.4.cloned.1.call-update
  7.3 0.7 convert_element_type.18
  8.0 1.1 %convert_element_type.17 = f32[64,4096]{1,0:T(8,128)S(1)} convert(bf16[64,4096]{1,0:T(8,128)(2,1)} %param.3) | non-fusion elementwise | flops 262144 | bytes 1572864 | tf_op jit(solution)/shard_map/convert_element_type | solution.py:33
  9.1 1.1 %multiply_convert_fusion = bf16[2,64,4096]{2,1,0:T(8,128)(2,1)} fusion(f32[2,4096]{1,0:T(2,128)S(1)} %convert_element_type.18, f32[64,4096]{1,0:T(8,128)S(1)} %convert_element_type.17), kind=kLoop, calls=%fused_computation.1 | loop fusion | flops 1048576 | bytes 2129920 | tf_op jit(solution)/shard_map/convert_element_type | solution.py:13
  10.3 24.0 %all-gather.4.cloned.1.call-done = bf16[256,4096]{1,0:T(8,128)(2,1)} async-done(((bf16[64,4096]{1,0:T(8,128)(2,1)}), bf16[256,4096]{1,0:T(8,128)(2,1)}) %all-gather.4.cloned.1.call-update) | async-done | bytes 2097168 | tf_op jit(solution)/shard_map/all_gather | solution.py:21
  34.2 0.0 copy-start
  34.2 2.9 %fusion.2 = f32[128,256]{1,0:T(8,128)S(1)} fusion(bf16[128,4096]{1,0:T(8,128)(2,1)} %bitcast.8, bf16[256,4096]{1,0:T(8,128)(2,1)} %all-gather.4.cloned.1.call-done), kind=kOutput, calls=%fused_computation.5 | convolution fusion | flops 268435456 | bytes 3276800 | tf_op jit(solution)/shard_map/rv,dv->rd/dot_general | solution.py:18
  37.1 38.3 %all-reduce.1 = bf16[128,256]{1,0:T(8,128)(2,1)S(1)} all-reduce(f32[128,256]{1,0:T(8,128)S(1)} %fusion.2), channel_id=1, replica_groups=mesh['blk'=4,'vox'=8] {'vox'}, use_global_device_ids=true, to_apply=%region_0.0 | all-reduce | flops 32768 | bytes 196608 | tf_op jit(solution)/shard_map/psum | solution.py:25
  75.5 0.0 copy-done
  75.5 0.5 multiply_reduce_fusion
  76.0 5.4 %all-gather.1 = f32[4,2,4096]{2,1,0:T(2,128)S(1)} all-gather(f32[1,2,4096]{2,1,0:T(2,128)S(1)} %bitcast.9), channel_id=2, replica_groups=mesh['blk'=4,'vox'=8] {'blk'}, dimensions={0}, use_global_device_ids=true | all-gather | bytes 163840 | tf_op jit(solution)/shard_map/all_gather | solution.py:34
  81.4 0.1 reduce_sum.19
  81.4 0.6 broadcast_multiply_fusion
Async XLA Ops:
  6.5 27.7 %all-gather.4.cloned.1.call-start = ((), (), s32[]{:S(2)}) async-start(), calls=%async_computation | async-start | bytes 2621440 | tf_op jit(solution)/shard_map/all_gather | solution.py:21
  34.2 41.2 %copy-start = (bf16[256,4096]{1,0:T(8,128)(2,1)S(1)}, bf16[256,4096]{1,0:T(8,128)(2,1)}, u32[]{:S(2)}) copy-start(bf16[256,4096]{1,0:T(8,128)(2,1)} %all-gather.4.cloned.1.call-done) | copy-start | bytes 6291460
Sparse Core Ops, SparseCore 0:
  8.9 25.2 all-gather.3
